TPU v7x, 32 devices: a whole 2x2x4 slice. The times are simulated.
32 devices in a mesh: zero: 8 (over z, x), model: 4 (over y, core).
Axes of the slice: x: 2, y: 2, z: 4, core: 2. Of those that a mesh axis runs over, the one named last changes fastest.
Arguments:
- w_query: bfloat16 [4096, 4096], P('zero', 'model'), may hold values from -0.125 to 0.125
- low_query: bfloat16 [4096, 16], P('zero'), may hold values from -0.09375 to 0.09375
- high_query: bfloat16 [16, 4096], P(None, 'model'), may hold values from -1.5 to 1.5
- w_key: bfloat16 [4096, 4096], P('zero', 'model'), may hold values from -0.125 to 0.125
- low_key: bfloat16 [4096, 16], P('zero'), may hold values from -0.09375 to 0.09375
- high_key: bfloat16 [16, 4096], P(None, 'model'), may hold values from -1.5 to 1.5
- w_value: bfloat16 [4096, 4096], P('zero', 'model'), may hold values from -0.125 to 0.125
- low_value: bfloat16 [4096, 16], P('zero'), may hold values from -0.09375 to 0.09375
- high_value: bfloat16 [16, 4096], P(None, 'model'), may hold values from -1.5 to 1.5
- norm_train: float32 [4096], P(('zero', 'model')), may hold values from 0.25 to 1.75
- norm_step: float32 [4096], P(('zero', 'model')), may hold values from -0.3 to 0.3
Outputs:
- serving_query: bfloat16 [4096, 4096], P(None, 'model')
- serving_key: bfloat16 [4096, 4096], P(None, 'model')
- serving_value: bfloat16 [4096, 4096], P(None, 'model')
- factor_query: float32 [4096], P('model')
- factor_key: float32 [4096], P('model')
- factor_value: float32 [4096], P('model')
- serve_norm: bfloat16 [4096], replicated
All inputs are finite; a program needn't handle non-finite values. Where the computation divides by a largest or mean magnitude, that divisor is 1e-20 or more.
Results may differ from a plain program's by a relative error of at most 0.001.
Values may be sent and summed in bfloat16 or wider, within the bound.
No kernel may reach another device: no remote copies, remote signals or barrier semaphores. Data moves between devices by JAX's collectives and lax.ppermute only.
A program may use at most 128 MiB of HBM per device.

v0:
```python
import jax
import jax.numpy as jnp
from jax import lax
from jax.sharding import PartitionSpec as P

D_MODEL = 4096


mix_rate = 0.5


def per_device(
    w_query,
    low_query,
    high_query,
    w_key,
    low_key,
    high_key,
    w_value,
    low_value,
    high_value,
    norm_train,
    norm_step,
):
    whole_query = w_query.astype(jnp.float32) + mix_rate * jnp.dot(
        low_query, high_query, preferred_element_type=jnp.float32
    )
    whole_key = w_key.astype(jnp.float32) + mix_rate * jnp.dot(
        low_key, high_key, preferred_element_type=jnp.float32
    )
    whole_value = w_value.astype(jnp.float32) + mix_rate * jnp.dot(
        low_value, high_value, preferred_element_type=jnp.float32
    )
    total_query, total_key, total_value = lax.psum(
        (
            jnp.sum(jnp.abs(whole_query), axis=0),
            jnp.sum(jnp.abs(whole_key), axis=0),
            jnp.sum(jnp.abs(whole_value), axis=0),
        ),
        "zero",
    )
    factor_query = total_query / D_MODEL
    factor_key = total_key / D_MODEL
    factor_value = total_value / D_MODEL
    narrow_query, narrow_key, narrow_value = (
        (whole_query / factor_query).astype(jnp.bfloat16),
        (whole_key / factor_key).astype(jnp.bfloat16),
        (whole_value / factor_value).astype(jnp.bfloat16),
    )
    serving_query, serving_key, serving_value = (
        lax.all_gather(narrow_query, "zero", axis=0, tiled=True),
        lax.all_gather(narrow_key, "zero", axis=0, tiled=True),
        lax.all_gather(narrow_value, "zero", axis=0, tiled=True),
    )
    serve_norm = lax.all_gather(
        (norm_train + norm_step).astype(jnp.bfloat16), ("zero", "model"), axis=0, tiled=True
    )
    return (
        serving_query,
        serving_key,
        serving_value,
        factor_query,
        factor_key,
        factor_value,
        serve_norm,
    )


def solution(mesh):
    placed = (
        P("zero", "model"),
        P("zero", None),
        P(None, "model"),
        P("zero", "model"),
        P("zero", None),
        P(None, "model"),
        P("zero", "model"),
        P("zero", None),
        P(None, "model"),
        P(("zero", "model")),
        P(("zero", "model")),
    )
    return jax.shard_map(
        per_device,
        mesh=mesh,
        in_specs=placed,
        out_specs=(
            P(None, "model"),
            P(None, "model"),
            P(None, "model"),
            P("model"),
            P("model"),
            P("model"),
            P(),
        ),
        check_vma=False,
    )
```

profile of v0, /device:TPU:0, one launch (start us, length us, event | category | flops | bytes accessed | tf_op | source)
XLA Modules:
  0.0 457.2 jit_solution(10498618471171676512)
XLA Ops:
  7.2 0.0 copy-start
  7.2 0.0 copy-start.1
  7.2 0.0 copy-start.5
  7.2 0.0 copy-start.3
  7.2 0.0 all-gather.7.cloned.1.call-start
  7.3 0.7 copy-done
  7.9 1.8 abs_reduce_fusion.2
  9.7 0.0 copy-done.1
  9.7 0.0 copy-done.5
  9.7 0.0 copy-done.3
  9.8 0.0 copy-start.2
  9.8 0.0 copy-start.4
  9.8 0.0 copy-start.6
  9.8 1.8 abs_reduce_fusion.1
  11.6 0.0 copy-done.2
  11.6 0.0 copy-done.4
  11.6 0.0 copy-done.6
  11.6 1.8 abs_reduce_fusion
  13.5 38.8 %all-reduce = (f32[1024]{0:T(1024)S(1)}, f32[1024]{0:T(1024)S(1)}, f32[1024]{0:T(1024)S(1)}) all-reduce(f32[1024]{0:T(1024)S(1)} %get-tuple-element.10, f32[1024]{0:T(1024)S(1)} %get-tuple-element.12, f32[1024]{0:T(1024)S(1)} %get-tuple-element.14), channel_id=1, replica_groups=mesh['zero'=8,'model'=4] {'zero'}, use_global_device_ids=true, to_apply=%region_1.0 | all-reduce | flops 3072 | bytes 24576 | tf_op jit(solution)/shard_map/psum | solution.py:34
  52.3 0.0 copy-start.7
  52.3 2.8 divide_convert_fusion.1
  55.1 0.0 all-gather.7.cloned.1.call-update
  55.2 0.0 copy-done.7
  55.2 0.0 all-gather.9.cloned.1.call-start
  55.2 0.0 copy-start.8
  55.2 2.9 divide_convert_fusion
  58.2 0.0 all-gather.9.cloned.1.call-update
  58.2 0.0 copy-done.8
  58.2 0.0 all-gather.5.cloned.1.call-start
  58.3 0.0 copy-start.9
  58.3 0.0 copy-start.10
  58.3 0.0 copy-start.11
  58.3 1.2 divide_convert_fusion.2
  59.5 0.0 all-gather.5.cloned.1.call-update
  59.6 0.0 copy-done.9
  59.6 0.0 copy-done.10
  59.6 0.0 copy-done.11
  59.6 39.3 %all-gather = bf16[32,1,128]{2,1,0:T(2,128)(2,1)S(1)} all-gather(bf16[1,1,128]{2,1,0:T(2,128)(2,1)S(1)} %convert_bitcast_fusion), channel_id=1, replica_groups=mesh['zero'=8,'model'=4] {'zero','model'}, dimensions={0}, use_global_device_ids=true | all-gather | bytes 8448 | tf_op jit(solution)/shard_map/all_gather | solution.py:55
  98.9 0.6 reduce
  99.5 77.6 %all-gather.7.cloned.1.call-done = bf16[4096,1024]{1,0:T(8,128)(2,1)} async-done(((bf16[512,1024]{1,0:T(8,128)(2,1)}), bf16[4096,1024]{1,0:T(8,128)(2,1)}) %all-gather.7.cloned.1.call-update) | async-done | bytes 8388624 | tf_op jit(solution)/shard_map/all_gather | solution.py:52
  177.1 124.8 %all-gather.9.cloned.1.call-done = bf16[4096,1024]{1,0:T(8,128)(2,1)} async-done(((bf16[512,1024]{1,0:T(8,128)(2,1)}), bf16[4096,1024]{1,0:T(8,128)(2,1)}) %all-gather.9.cloned.1.call-update) | async-done | bytes 8388624 | tf_op jit(solution)/shard_map/all_gather | solution.py:53
  302.0 125.4 %all-gather.5.cloned.1.call-done = bf16[4096,1024]{1,0:T(8,128)(2,1)} async-done(((bf16[512,1024]{1,0:T(8,128)(2,1)}), bf16[4096,1024]{1,0:T(8,128)(2,1)}) %all-gather.5.cloned.1.call-update) | async-done | bytes 8388624 | tf_op jit(solution)/shard_map/all_gather | solution.py:51
  427.4 7.8 %copy.21 = bf16[4096,1024]{1,0:T(8,128)(2,1)} copy(bf16[4096,1024]{1,0:T(8,128)(2,1)} %all-gather.5.cloned.1.call-done) | data formatting | bytes 16777216
  435.1 7.8 %copy.22 = bf16[4096,1024]{1,0:T(8,128)(2,1)} copy(bf16[4096,1024]{1,0:T(8,128)(2,1)} %all-gather.7.cloned.1.call-done) | data formatting | bytes 16777216
  442.9 7.8 %copy.23 = bf16[4096,1024]{1,0:T(8,128)(2,1)} copy(bf16[4096,1024]{1,0:T(8,128)(2,1)} %all-gather.9.cloned.1.call-done) | data formatting | bytes 16777216
  (4 shorter events, 0.0 us)
Async XLA Ops:
  7.2 0.8 copy-start
  7.2 2.5 copy-start.1
  7.2 2.5 copy-start.5
  7.2 2.5 copy-start.3
  7.2 169.9 %all-gather.7.cloned.1.call-start = ((), (), s32[]{:S(2)}) async-start(), calls=%async_computation.1 | async-start | bytes 9437184 | tf_op jit(solution)/shard_map/all_gather | solution.py:52
  9.8 1.9 copy-start.2
  9.8 1.9 copy-start.4
  9.8 1.9 copy-start.6
  52.3 2.8 copy-start.7
  55.2 246.8 %all-gather.9.cloned.1.call-start = ((), (), s32[]{:S(2)}) async-start(), calls=%async_computation.2 | async-start | bytes 9437184 | tf_op jit(solution)/shard_map/all_gather | solution.py:53
  55.2 3.0 copy-start.8
  58.2 369.2 %all-gather.5.cloned.1.call-start = ((), (), s32[]{:S(2)}) async-start(), calls=%async_computation | async-start | bytes 9437184 | tf_op jit(solution)/shard_map/all_gather | solution.py:51
  58.3 1.3 copy-start.9
  58.3 1.3 copy-start.10
  58.3 1.3 copy-start.11
Sparse Core Ops, SparseCore 0:
  55.3 121.8 all-gather.6
  179.3 122.6 all-gather.8
  304.7 122.6 all-gather.4
where the time goes:
time: 458 us; the launch traced here: 457 us
  waiting for transfers between devices  328 us (72%)
  blocking collectives  78.1 us (17%)
  local copies, waits for them, and re-layouts  24 us (5%)
  between operations  13.9 us (3%)
  other arithmetic  7.63 us (2%)
  matrix products  5.47 us (1%)
    all_gather x1, waiting for transfers between devices, per_device(): lax.all_gather(narrow_query, 'zero', axis=0, tiled=True)  125 us
    all_gather x1, waiting for transfers between devices, per_device(): lax.all_gather(narrow_value, 'zero', axis=0, tiled=True)  125 us
    all_gather x1, waiting for transfers between devices, per_device(): lax.all_gather(narrow_key, 'zero', axis=0, tiled=True)  77.6 us
    all_gather x1, blocking collectives, per_device(): lax.all_gather((norm_train + norm_step).astype(jnp.bfloat16), ('zero', 'm...  39.3 us
    psum x1, blocking collectives, per_device(): lax.psum((jnp.sum(jnp.abs(whole_query), axis=0), jnp.sum(jnp.abs(whole_ke...  38.8 us
    unnamed x27, local copies, waits for them, and re-layouts  24 us
  transfers between devices with their start and end apart: 3, of which 3 were waited for; matrix products, arithmetic and copies ran while one was open for 1% of the time, Pallas kernels for 0%

commit v1 on v0

v1 whole, which is shorter than its diff:
```python
import jax
import jax.numpy as jnp
from jax import lax
from jax.experimental import pallas as pl
from jax.experimental.pallas import tpu as pltpu
from jax.sharding import PartitionSpec as P


MIX_RATE = 0.5


HBM = pl.BlockSpec(memory_space=pl.ANY)
VMEM = pl.BlockSpec(memory_space=pltpu.VMEM)
SMEM = pl.BlockSpec(memory_space=pltpu.SMEM)


def merged_rows(held, extra, high, shape, s, h, r, step, column):
    _, rank = shape
    low_part = extra[s, h, :rank, column + r : column + r + step]
    product = lax.dot_general(
        low_part, high, (((0,), (0,)), ((), ())), preferred_element_type=jnp.float32
    )
    return held[s, h, r : r + step, :].astype(jnp.float32) + MIX_RATE * product


def finish(pieces, high, column, members, extra=None, partial=None, fresh=None, origin=None, norm=0):
    count = len(pieces)
    cols = pieces[0][0].shape[1]
    rank = high.shape[0]
    carried = extra is None
    half = pieces[0][0].shape[0] - (rank if carried else 0)
    step = min(128, half)
    full = origin is not None
    fresh = list(range(count)) if fresh is None else fresh

    operands = [p for pair in pieces for p in pair] + [high]
    specs = [HBM] * (2 * count) + [VMEM]
    for value, spec in ((extra, VMEM), (partial, VMEM), (origin, SMEM)):
        if value is not None:
            operands.append(value)
            specs.append(spec)
    if full:
        shapes = [
            jax.ShapeDtypeStruct((members * 2 * half, cols), jnp.bfloat16),
            jax.ShapeDtypeStruct((1, cols), jnp.float32),
        ]
        outs = [HBM, VMEM]
    else:
        shapes, outs = [jax.ShapeDtypeStruct((8, cols), jnp.float32)], [VMEM]
    if carried:
        shapes += [
            jax.ShapeDtypeStruct((members, 2, rank, cols), jnp.bfloat16),
            jax.ShapeDtypeStruct((members, norm), jnp.float32),
        ]
        outs += [VMEM, VMEM]
    scratch = [pltpu.VMEM((count, 2, half, cols), jnp.bfloat16), pltpu.SemaphoreType.DMA((count, 2))]
    if full:
        scratch += [
            pltpu.VMEM((len(fresh), 2, half, cols), jnp.float32),
            pltpu.SemaphoreType.DMA((count, 2)),
        ]
    if carried:
        scratch += [pltpu.SemaphoreType.DMA((count, 2))]

    def kernel(*refs):
        refs = list(refs)
        sources = [[refs.pop(0), refs.pop(0)] for _ in range(count)]
        high_ref = refs.pop(0)
        extra_ref = None if carried else refs.pop(0)
        partial_ref = refs.pop(0) if partial is not None else None
        origin_ref = refs.pop(0) if full else None
        if full:
            out, factor = refs.pop(0), refs.pop(0)
        else:
            total_ref = refs.pop(0)
        if carried:
            extra_ref, norm_ref = refs.pop(0), refs.pop(0)
        held, in_sems = refs.pop(0), refs.pop(0)
        if full:
            whole, out_sems = refs.pop(0), refs.pop(0)
        if carried:
            extra_sems = refs.pop(0)

        loads = {}
        for s in fresh + [s for s in range(count) if s not in fresh]:
            loads[s] = []
            for h in range(2):
                if carried:
                    loads[s].append(
                        pltpu.make_async_copy(
                            sources[s][h].at[pl.ds(half, rank)], extra_ref.at[s, h], extra_sems.at[s, h]
                        )
                    )
                loads[s].append(
                    pltpu.make_async_copy(
                        sources[s][h].at[pl.ds(0, half)], held.at[s, h], in_sems.at[s, h]
                    )
                )
            for copy in loads[s]:
                copy.start()
        high_part = high_ref[...]
        shape = (half, rank)
        total = jnp.zeros((8, cols), jnp.float32) if partial is None else partial_ref[...]
        for slot, s in enumerate(fresh):
            for copy in loads[s]:
                copy.wait()
            for h in range(2):
                for r in range(0, half, step):
                    value = merged_rows(held, extra_ref, high_part, shape, s, h, r, step, column)
                    if full:
                        whole[slot, h, r : r + step, :] = value
                    total = total + jnp.sum(jnp.abs(value).reshape(step // 8, 8, cols), axis=0)
        if not full:
            total_ref[...] = total
            return
        mean = jnp.sum(total, axis=0, keepdims=True) / (members * 2 * half)
        factor[...] = mean
        scale = 1.0 / mean
        stores = []
        for s in range(count):
            if s not in fresh:
                for copy in loads[s]:
                    copy.wait()
            for h in range(2):
                for r in range(0, half, step):
                    if s in fresh:
                        value = whole[fresh.index(s), h, r : r + step, :]
                    else:
                        value = merged_rows(held, extra_ref, high_part, shape, s, h, r, step, column)
                    held[s, h, r : r + step, :] = (value * scale).astype(jnp.bfloat16)
            first = pl.multiple_of(origin_ref[s] * (2 * half), 2 * half)
            pair = [
                pltpu.make_async_copy(
                    held.at[s, h], out.at[pl.ds(pl.multiple_of(first + h * half, half), half)], out_sems.at[s, h]
                )
                for h in range(2)
            ]
            stores.append(pair)
            for copy in pair:
                copy.start()
        if carried:
            spot = 3 * max(half, 128)
            for s in range(count):
                norm_ref[pl.ds(origin_ref[s], 1), :] = extra_ref[s, 0, 0:1, spot : spot + norm].astype(jnp.float32)
        for pair in stores:
            for copy in pair:
                copy.wait()

    return pl.pallas_call(
        kernel, out_shape=tuple(shapes), in_specs=specs, out_specs=tuple(outs), scratch_shapes=scratch
    )(*operands)


def after(value, *earlier):
    return lax.optimization_barrier((value, *earlier))[0]


def solution(mesh):
    members = mesh.shape["zero"]
    models = mesh.shape["model"]
    ring = list(range(0, members, 2)) + list(range(members - 1, 0, -2))
    place_of = [ring.index(m) for m in range(members)]
    onward = [(ring[p], ring[(p + 1) % members]) for p in range(members)]
    back = [(b, a) for a, b in onward]
    steps = members - 1
    lead = steps // 2
    turns = ["v", "q"] * lead + ["k", "q"] * (steps - lead) + ["v", "k"] * lead + ["v"]
    last = len(turns) - 1
    q_end = max(t for t, c in enumerate(turns) if c == "q")

    def per_device(
        w_query, low_query, high_query, w_key, low_key, high_key,
        w_value, low_value, high_value, norm_train, norm_step,
    ):
        rows, width = w_query.shape
        half = rows // 2
        rank = low_query.shape[1]
        stride = max(half, 128)
        norm_size = norm_train.shape[0]
        place = jnp.asarray(place_of, jnp.int32)[lax.axis_index("zero")]
        origin = jnp.asarray(ring, jnp.int32)[(place - jnp.arange(members)) % members]
        norm = (norm_train + norm_step).astype(jnp.bfloat16).reshape(1, -1)

        def below(h):
            parts = [low[h * half : (h + 1) * half].T for low in (low_query, low_key, low_value)]
            parts = [jnp.pad(p, ((0, 0), (0, stride - half))) for p in parts]
            parts.append(jnp.pad(norm, ((0, rank - 1), (0, width - 3 * stride - norm_size))))
            return jnp.concatenate(parts, axis=1)

        sent = {}
        sent["v"] = [[w_value[:half]], [w_value[half:]]]
        sent["q"] = [[jnp.concatenate([w_query[h * half : (h + 1) * half], below(h)], axis=0)] for h in range(2)]
        sent["k"] = [[w_key[:half]], [w_key[half:]]]

        def collected(c):
            top, bottom = sent[c]
            return [(top[s], bottom[(members - s) % members]) for s in range(members)]

        done = []
        result = {}
        last_at = {}
        for t, c in enumerate(turns):
            pair = (sent[c][0][-1], sent[c][1][-1])
            if t >= 2 and last_at.get(c) != t - 2:
                pair = after(pair, *done[t - 2])
            if t == q_end + 5:
                pair = after(pair, result["norm"])
            moved = lax.ppermute(pair[0], "zero", onward), lax.ppermute(pair[1], "zero", back)
            sent[c][0].append(moved[0])
            sent[c][1].append(moved[1])
            done.append(moved)
            last_at[c] = t
            if t == q_end:
                result["q"] = finish(collected("q"), high_query, 0, members, origin=origin, norm=norm_size)
                extra = result["q"][2]
                mine = lax.axis_index("model")
                near = result["q"][3].astype(jnp.bfloat16)
                gathered = [near] + [
                    lax.ppermute(near, "model", [(j, (j + m) % models) for j in range(models)])
                    for m in range(1, models)
                ]
                gathered = jnp.stack(gathered, axis=0)[(mine - jnp.arange(models)) % models]
                result["norm"] = jnp.swapaxes(gathered, 0, 1).reshape(-1)
            if t == last - 2:
                top, bottom = sent["v"]
                early = [s for s in range(members) if s not in (1, steps)]
                pieces = [(top[s], bottom[(members - s) % members]) for s in early]
                result["early"] = finish(
                    pieces, high_value, 2 * stride, members,
                    extra=jnp.concatenate([extra[0:1], extra[2:steps]], axis=0),
                )[0]
            if t == last - 1:
                result["k"] = finish(collected("k"), high_key, stride, members, extra=extra, origin=origin)
        result["v"] = finish(
            collected("v"), high_value, 2 * stride, members, extra=extra,
            partial=result["early"], fresh=[1, steps], origin=origin,
        )
        return (
            result["q"][0], result["k"][0], result["v"][0],
            result["q"][1].reshape(-1), result["k"][1].reshape(-1), result["v"][1].reshape(-1),
            result["norm"],
        )

    return jax.shard_map(
        per_device,
        mesh=mesh,
        in_specs=(
            P("zero", "model"), P("zero", None), P(None, "model"),
            P("zero", "model"), P("zero", None), P(None, "model"),
            P("zero", "model"), P("zero", None), P(None, "model"),
            P(("zero", "model")), P(("zero", "model")),
        ),
        out_specs=(
            P(None, "model"), P(None, "model"), P(None, "model"),
            P("model"), P("model"), P("model"), P(),
        ),
        check_vma=False,
    )
```

time: 458 us -> 263 us (0.57)
  waiting for transfers between devices: 328 us -> 167 us
  blocking collectives: 78.1 us -> 0 us
  starting transfers between devices: 0.12 us -> 47.4 us
  Pallas kernels: 0 us -> 36.7 us
  local copies, waits for them, and re-layouts: 24 us -> 6.46 us
  between operations: 13.9 us -> 1.39 us
  matrix products: 5.47 us -> 0 us
  other arithmetic: 7.63 us -> 2.94 us
    all_gather x3 -> x0, waiting for transfers between devices: 328 us -> none  [the longest x1 125 us: per_device(): lax.all_gather(narrow_query, 'zero', axis=0, tiled=True)]
    ppermute x0 -> x45, waiting for transfers between devices: none -> 167 us  [the longest x21 136 us: per_device(): lax.ppermute(pair[0], 'zero', onward)]
    ppermute x0 -> x45, starting transfers between devices: none -> 47.4 us  [the longest x21 42.1 us: per_device(): lax.ppermute(pair[0], 'zero', onward)]
    all_gather x1 -> x0, blocking collectives: 39.3 us -> none  [per_device(): lax.all_gather((norm_train + norm_step).astype(jnp.bfloat16), ('zero', 'm...]
    psum x1 -> x0, blocking collectives: 38.8 us -> none  [per_device(): lax.psum((jnp.sum(jnp.abs(whole_query), axis=0), jnp.sum(jnp.abs(whole_ke...]
    pallas_call x0 -> x4, Pallas kernels: none -> 36.7 us  [finish(): pl.pallas_call(kernel, out_shape=tuple(shapes), in_specs=specs, out_specs...]
    unnamed x27 -> x94, local copies, waits for them, and re-layouts: 24 us -> 0.2 us
    convert_element_type x3 -> x1, other arithmetic: 6.96 us -> 0.69 us  [per_device(): near = result['q'][3].astype(jnp.bfloat16)]
  transfers between devices with their start and end apart: 3 -> 45, of which waited for: 3 -> 25; matrix products, arithmetic and copies ran while one was open for 1% -> 3% of each run, Pallas kernels for 0% -> 11%
where the time goes in v1:
time: 263 us; the launch traced here: 262 us
  waiting for transfers between devices  167 us (63%)
  starting transfers between devices  47.4 us (18%)
  Pallas kernels  36.7 us (14%)
  local copies, waits for them, and re-layouts  6.46 us (2%)
  other arithmetic  2.94 us (1%)
    ppermute x21, waiting for transfers between devices, per_device(): lax.ppermute(pair[0], 'zero', onward)  136 us
    ppermute x21, starting transfers between devices, per_device(): lax.ppermute(pair[0], 'zero', onward)  42.1 us
    pallas_call x4, Pallas kernels, finish(): pl.pallas_call(kernel, out_shape=tuple(shapes), in_specs=specs, out_specs...  36.7 us
    ppermute x21, waiting for transfers between devices, per_device(): lax.ppermute(pair[1], 'zero', back)  28.7 us
  transfers between devices with their start and end apart: 45, of which 25 were waited for; matrix products, arithmetic and copies ran while one was open for 3% of the time, Pallas kernels for 11%

profile of v1, /device:TPU:0, one launch (start us, length us, event | category | flops | bytes accessed | tf_op | source)
XLA Modules:
  0.0 262.0 jit_solution(6683036938183973825)
XLA Ops:
  2.1 3.1 %collective-permute-start.14 = (bf16[256,1024]{1,0:T(8,128)(2,1)S(1)}, bf16[256,1024]{1,0:T(8,128)(2,1)S(1)}, u32[]{:S(2)}, u32[]{:S(2)}) collective-permute-start(bf16[256,1024]{1,0:T(8,128)(2,1)S(1)} %get-tuple-element.40.refs_0_), channel_id=1, source_target_pairs={{0,8},{8,16},{16,24},{24,28},{28,20},{20,12},{12,4},{4,0},{1,9},{9... | collective-permute-start | bytes 1572872 | tf_op jit(solution)/shard_map/ppermute | solution.py:208
  5.5 2.1 collective-permute-start
  7.6 10.3 %collective-permute-done.14.refs_2_ = bf16[256,1024]{1,0:T(8,128)(2,1)S(1)} collective-permute-done((bf16[256,1024]{1,0:T(8,128)(2,1)S(1)}, bf16[256,1024]{1,0:T(8,128)(2,1)S(1)}, u32[]{:S(2)}, u32[]{:S(2)}) %collective-permute-start.14) | collective-permute-done | bytes 524320 | tf_op jit(solution)/shard_map/ppermute | solution.py:208
  17.9 2.1 collective-permute-start.15
  20.0 9.8 %collective-permute-done.refs_2_ = bf16[272,1024]{1,0:T(8,128)(2,1)S(1)} collective-permute-done((bf16[272,1024]{1,0:T(8,128)(2,1)S(1)}, bf16[272,1024]{1,0:T(8,128)(2,1)S(1)}, u32[]{:S(2)}, u32[]{:S(2)}) %collective-permute-start) | collective-permute-done | bytes 557088 | tf_op jit(solution)/shard_map/ppermute | solution.py:208
  29.8 2.1 collective-permute-start.8
  31.9 9.1 %collective-permute-done.15.refs_2_.refs_4_ = bf16[256,1024]{1,0:T(8,128)(2,1)S(1)} collective-permute-done((bf16[256,1024]{1,0:T(8,128)(2,1)S(1)}, bf16[256,1024]{1,0:T(8,128)(2,1)S(1)}, u32[]{:S(2)}, u32[]{:S(2)}) %collective-permute-start.15) | collective-permute-done | bytes 524320 | tf_op jit(solution)/shard_map/ppermute | solution.py:208
  41.1 2.1 collective-permute-start.16
  43.2 9.8 %collective-permute-done.8.refs_4_ = bf16[272,1024]{1,0:T(8,128)(2,1)S(1)} collective-permute-done((bf16[272,1024]{1,0:T(8,128)(2,1)S(1)}, bf16[272,1024]{1,0:T(8,128)(2,1)S(1)}, u32[]{:S(2)}, u32[]{:S(2)}) %collective-permute-start.8) | collective-permute-done | bytes 557088 | tf_op jit(solution)/shard_map/ppermute | solution.py:208
  53.0 2.1 collective-permute-start.9
  55.3 8.9 %collective-permute-done.16.refs_4_.refs_6_ = bf16[256,1024]{1,0:T(8,128)(2,1)S(1)} collective-permute-done((bf16[256,1024]{1,0:T(8,128)(2,1)S(1)}, bf16[256,1024]{1,0:T(8,128)(2,1)S(1)}, u32[]{:S(2)}, u32[]{:S(2)}) %collective-permute-start.16) | collective-permute-done | bytes 524320 | tf_op jit(solution)/shard_map/ppermute | solution.py:208
  64.2 2.1 collective-permute-done.19.refs_9_.refs_11_
  66.3 1.6 collective-permute-start.20
  68.4 7.8 %collective-permute-done.9.refs_6_ = bf16[272,1024]{1,0:T(8,128)(2,1)S(1)} collective-permute-done((bf16[272,1024]{1,0:T(8,128)(2,1)S(1)}, bf16[272,1024]{1,0:T(8,128)(2,1)S(1)}, u32[]{:S(2)}, u32[]{:S(2)}) %collective-permute-start.9) | collective-permute-done | bytes 557088 | tf_op jit(solution)/shard_map/ppermute | solution.py:208
  76.2 2.1 collective-permute-start.10
  78.3 9.1 %collective-permute-done.20.refs_2_ = bf16[256,1024]{1,0:T(8,128)(2,1)S(1)} collective-permute-done((bf16[256,1024]{1,0:T(8,128)(2,1)S(1)}, bf16[256,1024]{1,0:T(8,128)(2,1)S(1)}, u32[]{:S(2)}, u32[]{:S(2)}) %collective-permute-start.20) | collective-permute-done | bytes 524320 | tf_op jit(solution)/shard_map/ppermute | solution.py:208
  87.4 2.1 collective-permute-start.21
  89.5 9.8 %collective-permute-done.10.refs_8_ = bf16[272,1024]{1,0:T(8,128)(2,1)S(1)} collective-permute-done((bf16[272,1024]{1,0:T(8,128)(2,1)S(1)}, bf16[272,1024]{1,0:T(8,128)(2,1)S(1)}, u32[]{:S(2)}, u32[]{:S(2)}) %collective-permute-start.10) | collective-permute-done | bytes 557088 | tf_op jit(solution)/shard_map/ppermute | solution.py:208
  99.3 2.1 collective-permute-start.11
  101.5 9.1 %collective-permute-done.21.refs_4_ = bf16[256,1024]{1,0:T(8,128)(2,1)S(1)} collective-permute-done((bf16[256,1024]{1,0:T(8,128)(2,1)S(1)}, bf16[256,1024]{1,0:T(8,128)(2,1)S(1)}, u32[]{:S(2)}, u32[]{:S(2)}) %collective-permute-start.21) | collective-permute-done | bytes 524320 | tf_op jit(solution)/shard_map/ppermute | solution.py:208
  110.6 2.1 collective-permute-start.22
  112.7 9.8 %collective-permute-done.11.refs_10_ = bf16[272,1024]{1,0:T(8,128)(2,1)S(1)} collective-permute-done((bf16[272,1024]{1,0:T(8,128)(2,1)S(1)}, bf16[272,1024]{1,0:T(8,128)(2,1)S(1)}, u32[]{:S(2)}, u32[]{:S(2)}) %collective-permute-start.11) | collective-permute-done | bytes 557088 | tf_op jit(solution)/shard_map/ppermute | solution.py:208
  122.5 2.1 collective-permute-start.12
  124.6 9.1 %collective-permute-done.22.refs_6_ = bf16[256,1024]{1,0:T(8,128)(2,1)S(1)} collective-permute-done((bf16[256,1024]{1,0:T(8,128)(2,1)S(1)}, bf16[256,1024]{1,0:T(8,128)(2,1)S(1)}, u32[]{:S(2)}, u32[]{:S(2)}) %collective-permute-start.22) | collective-permute-done | bytes 524320 | tf_op jit(solution)/shard_map/ppermute | solution.py:208
  133.7 2.1 collective-permute-start.23
  135.9 9.9 %collective-permute-done.12.refs_12_ = bf16[272,1024]{1,0:T(8,128)(2,1)} collective-permute-done((bf16[272,1024]{1,0:T(8,128)(2,1)S(1)}, bf16[272,1024]{1,0:T(8,128)(2,1)}, u32[]{:S(2)}, u32[]{:S(2)}) %collective-permute-start.12) | collective-permute-done | bytes 557088 | tf_op jit(solution)/shard_map/ppermute | solution.py:208
  145.8 2.1 collective-permute-start.13
  147.9 9.0 %collective-permute-done.23.refs_8_ = bf16[256,1024]{1,0:T(8,128)(2,1)S(1)} collective-permute-done((bf16[256,1024]{1,0:T(8,128)(2,1)S(1)}, bf16[256,1024]{1,0:T(8,128)(2,1)S(1)}, u32[]{:S(2)}, u32[]{:S(2)}) %collective-permute-start.23) | collective-permute-done | bytes 524320 | tf_op jit(solution)/shard_map/ppermute | solution.py:208
  156.9 2.1 collective-permute-done.27.refs_9_
  159.0 1.6 collective-permute-start.34
  163.7 5.3 %collective-permute-done.13.refs_14_ = bf16[272,1024]{1,0:T(8,128)(2,1)} collective-permute-done((bf16[272,1024]{1,0:T(8,128)(2,1)}, bf16[272,1024]{1,0:T(8,128)(2,1)}, u32[]{:S(2)}, u32[]{:S(2)}) %collective-permute-start.13) | collective-permute-done | bytes 557088 | tf_op jit(solution)/shard_map/ppermute | solution.py:208
  169.0 2.1 collective-permute-done.7.refs_3_
  171.1 11.1 %shard_map.180 = (bf16[4096,1024]{1,0:T(8,128)(2,1)}, f32[1,1024]{1,0:T(1,128)}, bf16[8,2,16,1024]{3,2,1,0:T(8,128)(2,1)}, f32[8,128]{1,0:T(8,128)}) custom-call(bf16[272,1024]{1,0:T(8,128)(2,1)} %copy-done.4, bf16[272,1024]{1,0:T(8,128)(2,1)} %copy-done.3, bf16[272,1024]{1,0:T(8,128)(2,1)} %copy-done.17, bf16[272,1024]{1,0:T(8,128)(2,1)} %collective-permute-done.7.refs_3_, ...), custom_call_target="tpu_custom_call" | custom-call | tf_op jit(solution)/shard_map/pallas_call | solution.py:149
  182.9 2.0 collective-permute-start.31
  184.9 1.6 collective-permute-start.35
  187.0 1.6 collective-permute-start.39
  188.5 2.1 collective-permute-done.39
  193.1 4.0 %collective-permute-done.28.refs_7_ = bf16[256,1024]{1,0:T(8,128)(2,1)} collective-permute-done((bf16[256,1024]{1,0:T(8,128)(2,1)S(1)}, bf16[256,1024]{1,0:T(8,128)(2,1)}, u32[]{:S(2)}, u32[]{:S(2)}) %collective-permute-start.28) | collective-permute-done | bytes 524320 | tf_op jit(solution)/shard_map/ppermute | solution.py:208
  197.1 2.3 collective-permute-start.32
  199.4 8.8 %collective-permute-done.35.refs_8_.refs_10_ = bf16[256,1024]{1,0:T(8,128)(2,1)S(1)} collective-permute-done((bf16[256,1024]{1,0:T(8,128)(2,1)}, bf16[256,1024]{1,0:T(8,128)(2,1)S(1)}, u32[]{:S(2)}, u32[]{:S(2)}) %collective-permute-start.35) | collective-permute-done | bytes 524320 | tf_op jit(solution)/shard_map/ppermute | solution.py:208
  208.3 2.3 collective-permute-start.41
  210.7 8.8 %collective-permute-done.29.refs_5_ = bf16[256,1024]{1,0:T(8,128)(2,1)S(1)} collective-permute-done((bf16[256,1024]{1,0:T(8,128)(2,1)}, bf16[256,1024]{1,0:T(8,128)(2,1)S(1)}, u32[]{:S(2)}, u32[]{:S(2)}) %collective-permute-start.29) | collective-permute-done | bytes 524320 | tf_op jit(solution)/shard_map/ppermute | solution.py:208
  219.5 2.3 collective-permute-start.33
  221.8 8.9 %collective-permute-done.41.refs_3_.refs_5_ = bf16[256,1024]{1,0:T(8,128)(2,1)S(1)} collective-permute-done((bf16[256,1024]{1,0:T(8,128)(2,1)S(1)}, bf16[256,1024]{1,0:T(8,128)(2,1)S(1)}, u32[]{:S(2)}, u32[]{:S(2)}) %collective-permute-start.41) | collective-permute-done | bytes 524320 | tf_op jit(solution)/shard_map/ppermute | solution.py:208
  230.7 2.3 collective-permute-start.44
  235.7 6.1 %shard_map.182.refs_18_ = f32[8,1024]{1,0:T(8,128)} custom-call(bf16[256,1024]{1,0:T(8,128)(2,1)} %copy-done.2, bf16[256,1024]{1,0:T(8,128)(2,1)} %copy-done.1, bf16[256,1024]{1,0:T(8,128)(2,1)} %copy-done.5, bf16[256,1024]{1,0:T(8,128)(2,1)} %copy-done.11, bf16[256,1024]{1,0:T(8,128)(2,1)} %copy-done.7, bf16[256,1024]{1,0:T(8,128)(2,1)} %copy-done.10, ...), custom_call_target="tpu_custom_call" | custom-call | tf_op jit(solution)/shard_map/pallas_call | solution.py:149
  242.1 11.0 %shard_map.181 = (bf16[4096,1024]{1,0:T(8,128)(2,1)}, f32[1,1024]{1,0:T(1,128)}) custom-call(bf16[256,1024]{1,0:T(8,128)(2,1)} %copy-done.14, bf16[256,1024]{1,0:T(8,128)(2,1)} %copy-done.13, bf16[256,1024]{1,0:T(8,128)(2,1)} %copy-done.29, bf16[256,1024]{1,0:T(8,128)(2,1)} %collective-permute-done.30.refs_3_, bf16[256,1024]{1,0:T(8,128)(2,1)} %copy-done.31, ...), custom_call_target="tpu_custom_call" | custom-call | tf_op jit(solution)/shard_map/pallas_call | solution.py:149
  253.3 8.6 %shard_map.183 = (bf16[4096,1024]{1,0:T(8,128)(2,1)}, f32[1,1024]{1,0:T(1,128)}) custom-call(bf16[256,1024]{1,0:T(8,128)(2,1)} %copy-done.2, bf16[256,1024]{1,0:T(8,128)(2,1)} %copy-done.1, bf16[256,1024]{1,0:T(8,128)(2,1)} %copy-done.27, bf16[256,1024]{1,0:T(8,128)(2,1)} %collective-permute-done.42.refs_3_, bf16[256,1024]{1,0:T(8,128)(2,1)} %copy-done.5, ...), custom_call_target="tpu_custom_call" | custom-call | tf_op jit(solution)/shard_map/pallas_call | solution.py:149
  (161 shorter events, 12.3 us)
Async XLA Ops:
  2.1 15.8 %collective-permute-start.14 = (bf16[256,1024]{1,0:T(8,128)(2,1)S(1)}, bf16[256,1024]{1,0:T(8,128)(2,1)S(1)}, u32[]{:S(2)}, u32[]{:S(2)}) collective-permute-start(bf16[256,1024]{1,0:T(8,128)(2,1)S(1)} %get-tuple-element.40.refs_0_), channel_id=1, source_target_pairs={{0,8},{8,16},{16,24},{24,28},{28,20},{20,12},{12,4},{4,0},{1,9},{9... | collective-permute-start | bytes 1572872 | tf_op jit(solution)/shard_map/ppermute | solution.py:208
  5.2 14.8 %collective-permute-start.17 = (bf16[256,1024]{1,0:T(8,128)(2,1)S(1)}, bf16[256,1024]{1,0:T(8,128)(2,1)S(1)}, u32[]{:S(2)}, u32[]{:S(2)}) collective-permute-start(bf16[256,1024]{1,0:T(8,128)(2,1)S(1)} %get-tuple-element.39.refs_1_), channel_id=1, source_target_pairs={{8,0},{16,8},{24,16},{28,24},{20,28},{12,20},{4,12},{0,4},{9,1},{1... | collective-permute-start | bytes 1572872 | tf_op jit(solution)/shard_map/ppermute | solution.py:208
  5.5 158.2 %copy-start.3 = (bf16[272,1024]{1,0:T(8,128)(2,1)}, bf16[272,1024]{1,0:T(8,128)(2,1)S(1)}, u32[]{:S(2)}) copy-start(bf16[272,1024]{1,0:T(8,128)(2,1)S(1)} %get-tuple-element.51.refs_1_) | copy-start | bytes 1671172
  5.5 158.2 %copy-start.4 = (bf16[272,1024]{1,0:T(8,128)(2,1)}, bf16[272,1024]{1,0:T(8,128)(2,1)S(1)}, u32[]{:S(2)}) copy-start(bf16[272,1024]{1,0:T(8,128)(2,1)S(1)} %get-tuple-element.52.refs_0_) | copy-start | bytes 1671172
  5.5 157.0 %copy-start = (s32[8]{0:T(128)S(1)}, s32[8]{0:T(128)}, u32[]{:S(2)}) copy-start(s32[8]{0:T(128)} %constant.50.clone) | copy-start | bytes 100
  5.5 24.3 %collective-permute-start = (bf16[272,1024]{1,0:T(8,128)(2,1)S(1)}, bf16[272,1024]{1,0:T(8,128)(2,1)S(1)}, u32[]{:S(2)}, u32[]{:S(2)}) collective-permute-start(bf16[272,1024]{1,0:T(8,128)(2,1)S(1)} %get-tuple-element.52.refs_0_), channel_id=1, source_target_pairs={{0,8},{8,16},{16,24},{24,28},{28,20},{20,12},{12,4},{4,0},{1,9},{9... | collective-permute-start | bytes 1671176 | tf_op jit(solution)/shard_map/ppermute | solution.py:208
  7.6 24.3 %collective-permute-start.1 = (bf16[272,1024]{1,0:T(8,128)(2,1)S(1)}, bf16[272,1024]{1,0:T(8,128)(2,1)S(1)}, u32[]{:S(2)}, u32[]{:S(2)}) collective-permute-start(bf16[272,1024]{1,0:T(8,128)(2,1)S(1)} %get-tuple-element.51.refs_1_), channel_id=1, source_target_pairs={{8,0},{16,8},{24,16},{28,24},{20,28},{12,20},{4,12},{0,4},{9,1},{1... | collective-permute-start | bytes 1671176 | tf_op jit(solution)/shard_map/ppermute | solution.py:208
  17.9 23.2 %collective-permute-start.15 = (bf16[256,1024]{1,0:T(8,128)(2,1)S(1)}, bf16[256,1024]{1,0:T(8,128)(2,1)S(1)}, u32[]{:S(2)}, u32[]{:S(2)}) collective-permute-start(bf16[256,1024]{1,0:T(8,128)(2,1)S(1)} %collective-permute-done.14.refs_2_), channel_id=1, source_target_pairs={{0,8},{8,16},{16,24},{24,28},{28,20},{20,12},{12,4},{4,0},{1,9},{9... | collective-permute-start | bytes 1572872 | tf_op jit(solution)/shard_map/ppermute | solution.py:208
  20.0 23.2 %collective-permute-start.18 = (bf16[256,1024]{1,0:T(8,128)(2,1)S(1)}, bf16[256,1024]{1,0:T(8,128)(2,1)S(1)}, u32[]{:S(2)}, u32[]{:S(2)}) collective-permute-start(bf16[256,1024]{1,0:T(8,128)(2,1)S(1)} %collective-permute-done.17.refs_15_), channel_id=1, source_target_pairs={{8,0},{16,8},{24,16},{28,24},{20,28},{12,20},{4,12},{0,4},{9,1},{1... | collective-permute-start | bytes 1572872 | tf_op jit(solution)/shard_map/ppermute | solution.py:208
  29.8 23.2 %collective-permute-start.8 = (bf16[272,1024]{1,0:T(8,128)(2,1)S(1)}, bf16[272,1024]{1,0:T(8,128)(2,1)S(1)}, u32[]{:S(2)}, u32[]{:S(2)}) collective-permute-start(bf16[272,1024]{1,0:T(8,128)(2,1)S(1)} %collective-permute-done.refs_2_), channel_id=1, source_target_pairs={{0,8},{8,16},{16,24},{24,28},{28,20},{20,12},{12,4},{4,0},{1,9},{9... | collective-permute-start | bytes 1671176 | tf_op jit(solution)/shard_map/ppermute | solution.py:208
  31.9 23.2 %collective-permute-start.2 = (bf16[272,1024]{1,0:T(8,128)(2,1)S(1)}, bf16[272,1024]{1,0:T(8,128)(2,1)S(1)}, u32[]{:S(2)}, u32[]{:S(2)}) collective-permute-start(bf16[272,1024]{1,0:T(8,128)(2,1)S(1)} %collective-permute-done.1.refs_15_), channel_id=1, source_target_pairs={{8,0},{16,8},{24,16},{28,24},{20,28},{12,20},{4,12},{0,4},{9,1},{1... | collective-permute-start | bytes 1671176 | tf_op jit(solution)/shard_map/ppermute | solution.py:208
  41.1 23.2 %collective-permute-start.16 = (bf16[256,1024]{1,0:T(8,128)(2,1)S(1)}, bf16[256,1024]{1,0:T(8,128)(2,1)S(1)}, u32[]{:S(2)}, u32[]{:S(2)}) collective-permute-start(bf16[256,1024]{1,0:T(8,128)(2,1)S(1)} %collective-permute-done.15.refs_2_.refs_4_), channel_id=1, source_target_pairs={{0,8},{8,16},{16,24},{24,28},{28,20},{20,12},{12,4},{4,0},{1,9},{9... | collective-permute-start | bytes 1572872 | tf_op jit(solution)/shard_map/ppermute | solution.py:208
  43.2 23.2 %collective-permute-start.19 = (bf16[256,1024]{1,0:T(8,128)(2,1)S(1)}, bf16[256,1024]{1,0:T(8,128)(2,1)S(1)}, u32[]{:S(2)}, u32[]{:S(2)}) collective-permute-start(bf16[256,1024]{1,0:T(8,128)(2,1)S(1)} %collective-permute-done.18.refs_11_.refs_13_), channel_id=1, source_target_pairs={{8,0},{16,8},{24,16},{28,24},{20,28},{12,20},{4,12},{0,4},{9,1},{1... | collective-permute-start | bytes 1572872 | tf_op jit(solution)/shard_map/ppermute | solution.py:208
  53.0 23.2 %collective-permute-start.9 = (bf16[272,1024]{1,0:T(8,128)(2,1)S(1)}, bf16[272,1024]{1,0:T(8,128)(2,1)S(1)}, u32[]{:S(2)}, u32[]{:S(2)}) collective-permute-start(bf16[272,1024]{1,0:T(8,128)(2,1)S(1)} %collective-permute-done.8.refs_4_), channel_id=1, source_target_pairs={{0,8},{8,16},{16,24},{24,28},{28,20},{20,12},{12,4},{4,0},{1,9},{9... | collective-permute-start | bytes 1671176 | tf_op jit(solution)/shard_map/ppermute | solution.py:208
  55.1 23.2 %collective-permute-start.3 = (bf16[272,1024]{1,0:T(8,128)(2,1)S(1)}, bf16[272,1024]{1,0:T(8,128)(2,1)S(1)}, u32[]{:S(2)}, u32[]{:S(2)}) collective-permute-start(bf16[272,1024]{1,0:T(8,128)(2,1)S(1)} %collective-permute-done.2.refs_13_), channel_id=1, source_target_pairs={{8,0},{16,8},{24,16},{28,24},{20,28},{12,20},{4,12},{0,4},{9,1},{1... | collective-permute-start | bytes 1671176 | tf_op jit(solution)/shard_map/ppermute | solution.py:208
  66.3 21.1 %collective-permute-start.20 = (bf16[256,1024]{1,0:T(8,128)(2,1)S(1)}, bf16[256,1024]{1,0:T(8,128)(2,1)S(1)}, u32[]{:S(2)}, u32[]{:S(2)}) collective-permute-start(bf16[256,1024]{1,0:T(8,128)(2,1)S(1)} %get-tuple-element.24.refs_0_), channel_id=1, source_target_pairs={{0,8},{8,16},{16,24},{24,28},{28,20},{20,12},{12,4},{4,0},{1,9},{9... | collective-permute-start | bytes 1572872 | tf_op jit(solution)/shard_map/ppermute | solution.py:208
  67.9 21.6 %collective-permute-start.24 = (bf16[256,1024]{1,0:T(8,128)(2,1)S(1)}, bf16[256,1024]{1,0:T(8,128)(2,1)S(1)}, u32[]{:S(2)}, u32[]{:S(2)}) collective-permute-start(bf16[256,1024]{1,0:T(8,128)(2,1)S(1)} %get-tuple-element.25.refs_1_), channel_id=1, source_target_pairs={{8,0},{16,8},{24,16},{28,24},{20,28},{12,20},{4,12},{0,4},{9,1},{1... | collective-permute-start | bytes 1572872 | tf_op jit(solution)/shard_map/ppermute | solution.py:208
  76.2 23.2 %collective-permute-start.10 = (bf16[272,1024]{1,0:T(8,128)(2,1)S(1)}, bf16[272,1024]{1,0:T(8,128)(2,1)S(1)}, u32[]{:S(2)}, u32[]{:S(2)}) collective-permute-start(bf16[272,1024]{1,0:T(8,128)(2,1)S(1)} %collective-permute-done.9.refs_6_), channel_id=1, source_target_pairs={{0,8},{8,16},{16,24},{24,28},{28,20},{20,12},{12,4},{4,0},{1,9},{9... | collective-permute-start | bytes 1671176 | tf_op jit(solution)/shard_map/ppermute | solution.py:208
  78.3 23.2 %collective-permute-start.4 = (bf16[272,1024]{1,0:T(8,128)(2,1)S(1)}, bf16[272,1024]{1,0:T(8,128)(2,1)S(1)}, u32[]{:S(2)}, u32[]{:S(2)}) collective-permute-start(bf16[272,1024]{1,0:T(8,128)(2,1)S(1)} %collective-permute-done.3.refs_11_), channel_id=1, source_target_pairs={{8,0},{16,8},{24,16},{28,24},{20,28},{12,20},{4,12},{0,4},{9,1},{1... | collective-permute-start | bytes 1671176 | tf_op jit(solution)/shard_map/ppermute | solution.py:208
  87.4 23.2 %collective-permute-start.21 = (bf16[256,1024]{1,0:T(8,128)(2,1)S(1)}, bf16[256,1024]{1,0:T(8,128)(2,1)S(1)}, u32[]{:S(2)}, u32[]{:S(2)}) collective-permute-start(bf16[256,1024]{1,0:T(8,128)(2,1)S(1)} %collective-permute-done.20.refs_2_), channel_id=1, source_target_pairs={{0,8},{8,16},{16,24},{24,28},{28,20},{20,12},{12,4},{4,0},{1,9},{9... | collective-permute-start | bytes 1572872 | tf_op jit(solution)/shard_map/ppermute | solution.py:208
  89.5 23.2 %collective-permute-start.25 = (bf16[256,1024]{1,0:T(8,128)(2,1)S(1)}, bf16[256,1024]{1,0:T(8,128)(2,1)S(1)}, u32[]{:S(2)}, u32[]{:S(2)}) collective-permute-start(bf16[256,1024]{1,0:T(8,128)(2,1)S(1)} %collective-permute-done.24.refs_15_), channel_id=1, source_target_pairs={{8,0},{16,8},{24,16},{28,24},{20,28},{12,20},{4,12},{0,4},{9,1},{1... | collective-permute-start | bytes 1572872 | tf_op jit(solution)/shard_map/ppermute | solution.py:208
  99.3 23.2 %collective-permute-start.11 = (bf16[272,1024]{1,0:T(8,128)(2,1)S(1)}, bf16[272,1024]{1,0:T(8,128)(2,1)S(1)}, u32[]{:S(2)}, u32[]{:S(2)}) collective-permute-start(bf16[272,1024]{1,0:T(8,128)(2,1)S(1)} %collective-permute-done.10.refs_8_), channel_id=1, source_target_pairs={{0,8},{8,16},{16,24},{24,28},{28,20},{20,12},{12,4},{4,0},{1,9},{9... | collective-permute-start | bytes 1671176 | tf_op jit(solution)/shard_map/ppermute | solution.py:208
  101.4 23.2 %collective-permute-start.5 = (bf16[272,1024]{1,0:T(8,128)(2,1)S(1)}, bf16[272,1024]{1,0:T(8,128)(2,1)S(1)}, u32[]{:S(2)}, u32[]{:S(2)}) collective-permute-start(bf16[272,1024]{1,0:T(8,128)(2,1)S(1)} %collective-permute-done.4.refs_9_), channel_id=1, source_target_pairs={{8,0},{16,8},{24,16},{28,24},{20,28},{12,20},{4,12},{0,4},{9,1},{1... | collective-permute-start | bytes 1671176 | tf_op jit(solution)/shard_map/ppermute | solution.py:208
  110.6 23.2 %collective-permute-start.22 = (bf16[256,1024]{1,0:T(8,128)(2,1)S(1)}, bf16[256,1024]{1,0:T(8,128)(2,1)S(1)}, u32[]{:S(2)}, u32[]{:S(2)}) collective-permute-start(bf16[256,1024]{1,0:T(8,128)(2,1)S(1)} %collective-permute-done.21.refs_4_), channel_id=1, source_target_pairs={{0,8},{8,16},{16,24},{24,28},{28,20},{20,12},{12,4},{4,0},{1,9},{9... | collective-permute-start | bytes 1572872 | tf_op jit(solution)/shard_map/ppermute | solution.py:208
  112.7 23.2 %collective-permute-start.26 = (bf16[256,1024]{1,0:T(8,128)(2,1)S(1)}, bf16[256,1024]{1,0:T(8,128)(2,1)S(1)}, u32[]{:S(2)}, u32[]{:S(2)}) collective-permute-start(bf16[256,1024]{1,0:T(8,128)(2,1)S(1)} %collective-permute-done.25.refs_13_), channel_id=1, source_target_pairs={{8,0},{16,8},{24,16},{28,24},{20,28},{12,20},{4,12},{0,4},{9,1},{1... | collective-permute-start | bytes 1572872 | tf_op jit(solution)/shard_map/ppermute | solution.py:208
  122.5 23.3 %collective-permute-start.12 = (bf16[272,1024]{1,0:T(8,128)(2,1)S(1)}, bf16[272,1024]{1,0:T(8,128)(2,1)}, u32[]{:S(2)}, u32[]{:S(2)}) collective-permute-start(bf16[272,1024]{1,0:T(8,128)(2,1)S(1)} %collective-permute-done.11.refs_10_), channel_id=1, source_target_pairs={{0,8},{8,16},{16,24},{24,28},{28,20},{20,12},{12,4},{4,0},{1,9},{9... | collective-permute-start | bytes 1671176 | tf_op jit(solution)/shard_map/ppermute | solution.py:208
  124.6 23.3 %collective-permute-start.6 = (bf16[272,1024]{1,0:T(8,128)(2,1)S(1)}, bf16[272,1024]{1,0:T(8,128)(2,1)}, u32[]{:S(2)}, u32[]{:S(2)}) collective-permute-start(bf16[272,1024]{1,0:T(8,128)(2,1)S(1)} %collective-permute-done.5.refs_7_), channel_id=1, source_target_pairs={{8,0},{16,8},{24,16},{28,24},{20,28},{12,20},{4,12},{0,4},{9,1},{1... | collective-permute-start | bytes 1671176 | tf_op jit(solution)/shard_map/ppermute | solution.py:208
  133.7 23.2 %collective-permute-start.23 = (bf16[256,1024]{1,0:T(8,128)(2,1)S(1)}, bf16[256,1024]{1,0:T(8,128)(2,1)S(1)}, u32[]{:S(2)}, u32[]{:S(2)}) collective-permute-start(bf16[256,1024]{1,0:T(8,128)(2,1)S(1)} %collective-permute-done.22.refs_6_), channel_id=1, source_target_pairs={{0,8},{8,16},{16,24},{24,28},{28,20},{20,12},{12,4},{4,0},{1,9},{9... | collective-permute-start | bytes 1572872 | tf_op jit(solution)/shard_map/ppermute | solution.py:208
  135.9 23.2 %collective-permute-start.27 = (bf16[256,1024]{1,0:T(8,128)(2,1)S(1)}, bf16[256,1024]{1,0:T(8,128)(2,1)S(1)}, u32[]{:S(2)}, u32[]{:S(2)}) collective-permute-start(bf16[256,1024]{1,0:T(8,128)(2,1)S(1)} %collective-permute-done.26.refs_11_), channel_id=1, source_target_pairs={{8,0},{16,8},{24,16},{28,24},{20,28},{12,20},{4,12},{0,4},{9,1},{1... | collective-permute-start | bytes 1572872 | tf_op jit(solution)/shard_map/ppermute | solution.py:208
  145.8 23.2 %collective-permute-start.13 = (bf16[272,1024]{1,0:T(8,128)(2,1)}, bf16[272,1024]{1,0:T(8,128)(2,1)}, u32[]{:S(2)}, u32[]{:S(2)}) collective-permute-start(bf16[272,1024]{1,0:T(8,128)(2,1)} %collective-permute-done.12.refs_12_), channel_id=1, source_target_pairs={{0,8},{8,16},{16,24},{24,28},{28,20},{20,12},{12,4},{4,0},{1,9},{9... | collective-permute-start | bytes 1671176 | tf_op jit(solution)/shard_map/ppermute | solution.py:208
  147.9 23.2 %collective-permute-start.7 = (bf16[272,1024]{1,0:T(8,128)(2,1)}, bf16[272,1024]{1,0:T(8,128)(2,1)}, u32[]{:S(2)}, u32[]{:S(2)}) collective-permute-start(bf16[272,1024]{1,0:T(8,128)(2,1)} %collective-permute-done.6.refs_5_), channel_id=1, source_target_pairs={{8,0},{16,8},{24,16},{28,24},{20,28},{12,20},{4,12},{0,4},{9,1},{1... | collective-permute-start | bytes 1671176 | tf_op jit(solution)/shard_map/ppermute | solution.py:208
  159.0 25.9 %collective-permute-start.34 = (bf16[256,1024]{1,0:T(8,128)(2,1)S(1)}, bf16[256,1024]{1,0:T(8,128)(2,1)}, u32[]{:S(2)}, u32[]{:S(2)}) collective-permute-start(bf16[256,1024]{1,0:T(8,128)(2,1)S(1)} %collective-permute-done.16.refs_4_.refs_6_), channel_id=1, source_target_pairs={{0,8},{8,16},{16,24},{24,28},{28,20},{20,12},{12,4},{4,0},{1,9},{9... | collective-permute-start | bytes 1572872 | tf_op jit(solution)/shard_map/ppermute | solution.py:208
  160.6 25.9 %collective-permute-start.36 = (bf16[256,1024]{1,0:T(8,128)(2,1)S(1)}, bf16[256,1024]{1,0:T(8,128)(2,1)}, u32[]{:S(2)}, u32[]{:S(2)}) collective-permute-start(bf16[256,1024]{1,0:T(8,128)(2,1)S(1)} %collective-permute-done.19.refs_9_.refs_11_), channel_id=1, source_target_pairs={{8,0},{16,8},{24,16},{28,24},{20,28},{12,20},{4,12},{0,4},{9,1},{1... | collective-permute-start | bytes 1572872 | tf_op jit(solution)/shard_map/ppermute | solution.py:208
  182.9 4.1 %collective-permute-start.38 = (bf16[8,128]{1,0:T(8,128)(2,1)S(1)}, bf16[8,128]{1,0:T(8,128)(2,1)S(1)}, u32[]{:S(2)}, u32[]{:S(2)}) collective-permute-start(bf16[8,128]{1,0:T(8,128)(2,1)S(1)} %convert_element_type.10), channel_id=1, source_target_pairs={{0,1},{1,2},{2,3},{3,0},{4,5},{5,6},{6,7},{7,4},{8,9},{9,10},{10,1... | collective-permute-start | bytes 6152 | tf_op jit(solution)/shard_map/ppermute | solution.py:219
  182.9 14.3 %collective-permute-start.28 = (bf16[256,1024]{1,0:T(8,128)(2,1)S(1)}, bf16[256,1024]{1,0:T(8,128)(2,1)}, u32[]{:S(2)}, u32[]{:S(2)}) collective-permute-start(bf16[256,1024]{1,0:T(8,128)(2,1)S(1)} %copy-done.38), channel_id=1, source_target_pairs={{8,0},{16,8},{24,16},{28,24},{20,28},{12,20},{4,12},{0,4},{9,1},{1... | collective-permute-start | bytes 1572872 | tf_op jit(solution)/shard_map/ppermute | solution.py:208
  182.9 14.2 %collective-permute-start.31 = (bf16[256,1024]{1,0:T(8,128)(2,1)S(1)}, bf16[256,1024]{1,0:T(8,128)(2,1)}, u32[]{:S(2)}, u32[]{:S(2)}) collective-permute-start(bf16[256,1024]{1,0:T(8,128)(2,1)S(1)} %copy-done.36), channel_id=1, source_target_pairs={{0,8},{8,16},{16,24},{24,28},{28,20},{20,12},{12,4},{4,0},{1,9},{9... | collective-permute-start | bytes 1572872 | tf_op jit(solution)/shard_map/ppermute | solution.py:208
  184.9 23.3 %collective-permute-start.35 = (bf16[256,1024]{1,0:T(8,128)(2,1)}, bf16[256,1024]{1,0:T(8,128)(2,1)S(1)}, u32[]{:S(2)}, u32[]{:S(2)}) collective-permute-start(bf16[256,1024]{1,0:T(8,128)(2,1)} %collective-permute-done.34.refs_6_.refs_8_), channel_id=1, source_target_pairs={{0,8},{8,16},{16,24},{24,28},{28,20},{20,12},{12,4},{4,0},{1,9},{9... | collective-permute-start | bytes 1572872 | tf_op jit(solution)/shard_map/ppermute | solution.py:208
  186.5 21.8 %collective-permute-start.37 = (bf16[256,1024]{1,0:T(8,128)(2,1)}, bf16[256,1024]{1,0:T(8,128)(2,1)S(1)}, u32[]{:S(2)}, u32[]{:S(2)}) collective-permute-start(bf16[256,1024]{1,0:T(8,128)(2,1)} %collective-permute-done.36.refs_7_.refs_9_), channel_id=1, source_target_pairs={{8,0},{16,8},{24,16},{28,24},{20,28},{12,20},{4,12},{0,4},{9,1},{1... | collective-permute-start | bytes 1572872 | tf_op jit(solution)/shard_map/ppermute | solution.py:208
  187.0 3.7 %collective-permute-start.39 = (bf16[8,128]{1,0:T(8,128)(2,1)S(1)}, bf16[8,128]{1,0:T(8,128)(2,1)S(1)}, u32[]{:S(2)}, u32[]{:S(2)}) collective-permute-start(bf16[8,128]{1,0:T(8,128)(2,1)S(1)} %convert_element_type.10), channel_id=1, source_target_pairs={{0,2},{1,3},{2,0},{3,1},{4,6},{5,7},{6,4},{7,5},{8,10},{9,11},{10,... | collective-permute-start | bytes 6152 | tf_op jit(solution)/shard_map/ppermute | solution.py:219
  190.6 1.3 collective-permute-start.40
  197.1 22.4 %collective-permute-start.29 = (bf16[256,1024]{1,0:T(8,128)(2,1)}, bf16[256,1024]{1,0:T(8,128)(2,1)S(1)}, u32[]{:S(2)}, u32[]{:S(2)}) collective-permute-start(bf16[256,1024]{1,0:T(8,128)(2,1)} %collective-permute-done.28.refs_7_), channel_id=1, source_target_pairs={{8,0},{16,8},{24,16},{28,24},{20,28},{12,20},{4,12},{0,4},{9,1},{1... | collective-permute-start | bytes 1572872 | tf_op jit(solution)/shard_map/ppermute | solution.py:208
  197.1 22.4 %collective-permute-start.32 = (bf16[256,1024]{1,0:T(8,128)(2,1)}, bf16[256,1024]{1,0:T(8,128)(2,1)S(1)}, u32[]{:S(2)}, u32[]{:S(2)}) collective-permute-start(bf16[256,1024]{1,0:T(8,128)(2,1)} %collective-permute-done.31.refs_10_), channel_id=1, source_target_pairs={{0,8},{8,16},{16,24},{24,28},{28,20},{20,12},{12,4},{4,0},{1,9},{9... | collective-permute-start | bytes 1572872 | tf_op jit(solution)/shard_map/ppermute | solution.py:208
  208.3 22.5 %collective-permute-start.41 = (bf16[256,1024]{1,0:T(8,128)(2,1)S(1)}, bf16[256,1024]{1,0:T(8,128)(2,1)S(1)}, u32[]{:S(2)}, u32[]{:S(2)}) collective-permute-start(bf16[256,1024]{1,0:T(8,128)(2,1)S(1)} %collective-permute-done.37.refs_5_.refs_7_), channel_id=1, source_target_pairs={{8,0},{16,8},{24,16},{28,24},{20,28},{12,20},{4,12},{0,4},{9,1},{1... | collective-permute-start | bytes 1572872 | tf_op jit(solution)/shard_map/ppermute | solution.py:208
  210.5 20.2 %collective-permute-start.43 = (bf16[256,1024]{1,0:T(8,128)(2,1)S(1)}, bf16[256,1024]{1,0:T(8,128)(2,1)S(1)}, u32[]{:S(2)}, u32[]{:S(2)}) collective-permute-start(bf16[256,1024]{1,0:T(8,128)(2,1)S(1)} %collective-permute-done.35.refs_8_.refs_10_), channel_id=1, source_target_pairs={{0,8},{8,16},{16,24},{24,28},{28,20},{20,12},{12,4},{4,0},{1,9},{9... | collective-permute-start | bytes 1572872 | tf_op jit(solution)/shard_map/ppermute | solution.py:208
  219.5 22.6 %collective-permute-start.30 = (bf16[256,1024]{1,0:T(8,128)(2,1)S(1)}, bf16[256,1024]{1,0:T(8,128)(2,1)}, u32[]{:S(2)}, u32[]{:S(2)}) collective-permute-start(bf16[256,1024]{1,0:T(8,128)(2,1)S(1)} %collective-permute-done.29.refs_5_), channel_id=1, source_target_pairs={{8,0},{16,8},{24,16},{28,24},{20,28},{12,20},{4,12},{0,4},{9,1},{1... | collective-permute-start | bytes 1572872 | tf_op jit(solution)/shard_map/ppermute | solution.py:208
  219.5 22.6 %collective-permute-start.33 = (bf16[256,1024]{1,0:T(8,128)(2,1)S(1)}, bf16[256,1024]{1,0:T(8,128)(2,1)}, u32[]{:S(2)}, u32[]{:S(2)}) collective-permute-start(bf16[256,1024]{1,0:T(8,128)(2,1)S(1)} %collective-permute-done.32.refs_12_), channel_id=1, source_target_pairs={{0,8},{8,16},{16,24},{24,28},{28,20},{20,12},{12,4},{4,0},{1,9},{9... | collective-permute-start | bytes 1572872 | tf_op jit(solution)/shard_map/ppermute | solution.py:208
  230.7 22.6 %collective-permute-start.42 = (bf16[256,1024]{1,0:T(8,128)(2,1)S(1)}, bf16[256,1024]{1,0:T(8,128)(2,1)}, u32[]{:S(2)}, u32[]{:S(2)}) collective-permute-start(bf16[256,1024]{1,0:T(8,128)(2,1)S(1)} %collective-permute-done.41.refs_3_.refs_5_), channel_id=1, source_target_pairs={{8,0},{16,8},{24,16},{28,24},{20,28},{12,20},{4,12},{0,4},{9,1},{1... | collective-permute-start | bytes 1572872 | tf_op jit(solution)/shard_map/ppermute | solution.py:208
  230.7 22.6 %collective-permute-start.44 = (bf16[256,1024]{1,0:T(8,128)(2,1)S(1)}, bf16[256,1024]{1,0:T(8,128)(2,1)}, u32[]{:S(2)}, u32[]{:S(2)}) collective-permute-start(bf16[256,1024]{1,0:T(8,128)(2,1)S(1)} %collective-permute-done.43.refs_10_.refs_12_), channel_id=1, source_target_pairs={{0,8},{8,16},{16,24},{24,28},{28,20},{20,12},{12,4},{4,0},{1,9},{9... | collective-permute-start | bytes 1572872 | tf_op jit(solution)/shard_map/ppermute | solution.py:208
  (44 other events, 2271.0 us)
